TPU v7x, 32 devices: a whole 2x2x4 slice. The times are simulated.
32 devices in a mesh: band: 8 (over z, x), patch: 4 (over y, core).
Axes of the slice: x: 2, y: 2, z: 4, core: 2. Of those that a mesh axis runs over, the one named last changes fastest.
Arguments:
- latents: bfloat16 [8, 10240, 512], P('band', 'patch'), may hold values from -6 to 6
- owners: int32 [16], replicated, may hold values from 0 to 3, as said below
- block_rows: int32 [16, 128], replicated, may hold values from 0 to 2559
- interp_weights: bfloat16 [16, 1024, 128], P('band', 'patch'), may hold values from -0.5 to 0.5
- w_first: bfloat16 [8, 512, 512], P('band'), may hold values from -0.25 to 0.25
- b_first: float32 [8, 512], P('band'), may hold values from -3 to 3
- w_second: bfloat16 [8, 512, 512], P('band'), may hold values from -0.25 to 0.25
- b_second: float32 [8, 512], P('band'), may hold values from -4 to 4
- gain: float32 [8, 512], P('band'), may hold values from 0.1 to 1.9
- w_out: bfloat16 [8, 12, 512], P('band'), may hold values from -0.25 to 0.25
- b_out: float32 [8, 12], P('band'), may hold values from -4 to 4
Outputs:
- grid_fields: float32 [8, 12, 16384], P('band', None, 'patch')
Inputs may be any that keep to these rules, and one draw needn't show every extreme that they name: `owners`: no patch owns more than 8 tiles, and one patch owns exactly 8.
All inputs are finite; a program needn't handle non-finite values.
Results may differ from a plain program's by a relative error of at most 0.003.
Values may be sent and summed in bfloat16 or wider, within the bound.
A program may use at most 64 MiB of HBM per device.

v0:
```python
import jax
import jax.numpy as jnp
from jax import lax
from jax.sharding import PartitionSpec as P


def decode_rows(interp, w_first, b_first, w_second, b_second, gain, w_out, b_out):
    hidden = jax.nn.silu(
        jnp.dot(interp, w_first, preferred_element_type=jnp.float32) + b_first
    ).astype(jnp.bfloat16)
    second = jnp.dot(hidden, w_second, preferred_element_type=jnp.float32) + b_second
    mean_value = jnp.mean(second, axis=-1, keepdims=True)
    centred = second - mean_value
    variance = jnp.mean(centred * centred, axis=-1, keepdims=True)
    normed = (centred * lax.rsqrt(variance + 1e-05) * gain).astype(jnp.bfloat16)
    result = lax.dot_general(
        w_out, normed, (((1,), (1,)), ((), ())), preferred_element_type=jnp.float32
    )
    return result + b_out[:, None]


def body(
    latents,
    owners,
    block_rows,
    interp_weights,
    w_first,
    b_first,
    w_second,
    b_second,
    gain,
    w_out,
    b_out,
):
    tile_count = owners.shape[0]
    cell_count = interp_weights.shape[1]
    channels = w_out.shape[1]
    local_latents = latents[0]
    width = local_latents.shape[1]
    weights_all = lax.all_gather(interp_weights, "band", axis=0, tiled=True)

    def decode_tile(tile_index, block):
        tile_weights = lax.dynamic_index_in_dim(weights_all, tile_index, 0, keepdims=False)
        interp = jnp.dot(tile_weights, block, preferred_element_type=jnp.float32).astype(
            jnp.bfloat16
        )
        return decode_rows(
            interp, w_first[0], b_first[0], w_second[0], b_second[0], gain[0], w_out[0], b_out[0]
        )

    empty = jnp.zeros((channels, tile_count, cell_count), jnp.float32)
    my_index = lax.axis_index("patch")
    own_tiles = jnp.take(local_latents, block_rows.reshape(-1), axis=0).reshape(
        tile_count, -1, width
    )
    mine = (owners == my_index)[:, None, None]
    filled = jnp.where(mine, own_tiles.astype(jnp.float32), jnp.float32(0.0))
    all_blocks = lax.psum(filled.astype(jnp.bfloat16), "patch")

    def visit_summed(turn_index, buffer):
        tile_index = turn_index % tile_count
        block = lax.dynamic_index_in_dim(all_blocks, tile_index, 0, keepdims=False)
        result = decode_tile(tile_index, block)
        return lax.dynamic_update_index_in_dim(buffer, result, tile_index, 1)

    decoded = lax.fori_loop(0, tile_count, visit_summed, empty)
    regrid = lax.all_to_all(decoded, "patch", split_axis=1, concat_axis=2, tiled=True)
    return regrid.reshape(channels, -1)[None]


def solution(mesh):
    return jax.shard_map(
        body,
        mesh=mesh,
        in_specs=(
            P("band", "patch", None),
            P(),
            P(),
            P("band", "patch", None),
            P("band", None, None),
            P("band", None),
            P("band", None, None),
            P("band", None),
            P("band", None),
            P("band", None, None),
            P("band", None),
        ),
        out_specs=P("band", None, "patch"),
        check_vma=False,
    )
```

profile of v0, /device:TPU:0, one launch (start us, length us, event | category | flops | bytes accessed | tf_op | source)
XLA Modules:
  0.0 144.4 jit_solution(14935995324864705536)
XLA Ops:
  9.1 9.2 %gather_fusion = bf16[2048,512]{1,0:T(8,128)(2,1)} fusion(bf16[2560,512]{1,0:T(8,128)(2,1)S(1)} %bitcast.62, s32[2048]{0:T(1024)S(1)} %broadcast_clamp_fusion), kind=kCustom, calls=%fused_computation | custom fusion | bytes 4202496 | tf_op jit(solution)/shard_map/jit(_take)/gather | solution.py:53
  18.3 2.9 %select_convert_fusion = bf16[16,128,512]{2,1,0:T(8,128)(2,1)} fusion(bf16[16,128,512]{2,1,0:T(8,128)(2,1)} %bitcast.63, pred[16]{0:T(512)(128)(4,1)S(1)} %broadcast_compare_fusion, pred[16,128]{1,0:T(8,128)(4,1)S(1)} %compare_and_fusion), kind=kLoop, calls=%fused_computation.23 | loop fusion | flops 4194304 | bytes 4196368 | tf_op jit(solution)/shard_map/convert_element_type | solution.py:58
  21.9 53.7 %all-reduce.2.cloned.1.call-done = bf16[16,128,512]{2,1,0:T(8,128)(2,1)} async-done(((bf16[16,128,512]{2,1,0:T(8,128)(2,1)}), bf16[16,128,512]{2,1,0:T(8,128)(2,1)}) %all-reduce.2.cloned.1.call-update) | async-done | bytes 2097168 | tf_op jit(solution)/shard_map/psum | solution.py:58
  76.3 50.2 %while.15 = (s32[]{:T(128)}, f32[12,16,256]{2,0,1:T(8,128)}, bf16[16,256,128]{2,1,0:T(8,128)(2,1)}, bf16[16,128,512]{2,1,0:T(8,128)(2,1)}, bf16[1,512,512]{2,1,0...) while((s32[]{:T(128)}, f32[12,16,256]{2,0,1:T(8,128)}, ...), condition=%wide.region_4.5_spmd, body=%wide.region_1.4_spmd.sunk | while | flops 307236096 | bytes 3387677 | solution.py:66
  76.3 1.7 %multiply_convert_fusion.6 = bf16[256,512]{1,0:T(8,128)(2,1)S(1)} fusion(bf16[1,512,512]{2,1,0:T(8,128)(2,1)} %get-tuple-element.400, f32[512]{0:T(512)S(1)} %bitcast.71, bf16[16,128,512]{2,1,0:T(8,128)(2,1)} %get-tuple-element.399, s32[]{:T(128)S(6)} %select_n.74, bf16[16,256,128]{2,1,0:T(8,128)(2,1)} %get-tuple-element.398), kind=kOutput, calls=%fused_computation.11.clone.1 | convolution fusion | flops 168689664 | bytes 986112 | tf_op jit(solution)/shard_map/while/body/eval_jaxpr/dot_general | solution.py:9
  79.5 1.6 %multiply_convert_fusion.6 = bf16[256,512]{1,0:T(8,128)(2,1)S(1)} fusion(bf16[1,512,512]{2,1,0:T(8,128)(2,1)} %get-tuple-element.400, f32[512]{0:T(512)S(1)} %bitcast.71, bf16[16,128,512]{2,1,0:T(8,128)(2,1)} %get-tuple-element.399, s32[]{:T(128)S(6)} %select_n.74, bf16[16,256,128]{2,1,0:T(8,128)(2,1)} %get-tuple-element.398), kind=kOutput, calls=%fused_computation.11.clone.1 | convolution fusion | flops 168689664 | bytes 986112 | tf_op jit(solution)/shard_map/while/body/eval_jaxpr/dot_general | solution.py:9
  82.6 1.6 %multiply_convert_fusion.6 = bf16[256,512]{1,0:T(8,128)(2,1)S(1)} fusion(bf16[1,512,512]{2,1,0:T(8,128)(2,1)} %get-tuple-element.400, f32[512]{0:T(512)S(1)} %bitcast.71, bf16[16,128,512]{2,1,0:T(8,128)(2,1)} %get-tuple-element.399, s32[]{:T(128)S(6)} %select_n.74, bf16[16,256,128]{2,1,0:T(8,128)(2,1)} %get-tuple-element.398), kind=kOutput, calls=%fused_computation.11.clone.1 | convolution fusion | flops 168689664 | bytes 986112 | tf_op jit(solution)/shard_map/while/body/eval_jaxpr/dot_general | solution.py:9
  85.7 1.6 %multiply_convert_fusion.6 = bf16[256,512]{1,0:T(8,128)(2,1)S(1)} fusion(bf16[1,512,512]{2,1,0:T(8,128)(2,1)} %get-tuple-element.400, f32[512]{0:T(512)S(1)} %bitcast.71, bf16[16,128,512]{2,1,0:T(8,128)(2,1)} %get-tuple-element.399, s32[]{:T(128)S(6)} %select_n.74, bf16[16,256,128]{2,1,0:T(8,128)(2,1)} %get-tuple-element.398), kind=kOutput, calls=%fused_computation.11.clone.1 | convolution fusion | flops 168689664 | bytes 986112 | tf_op jit(solution)/shard_map/while/body/eval_jaxpr/dot_general | solution.py:9
  88.9 1.6 %multiply_convert_fusion.6 = bf16[256,512]{1,0:T(8,128)(2,1)S(1)} fusion(bf16[1,512,512]{2,1,0:T(8,128)(2,1)} %get-tuple-element.400, f32[512]{0:T(512)S(1)} %bitcast.71, bf16[16,128,512]{2,1,0:T(8,128)(2,1)} %get-tuple-element.399, s32[]{:T(128)S(6)} %select_n.74, bf16[16,256,128]{2,1,0:T(8,128)(2,1)} %get-tuple-element.398), kind=kOutput, calls=%fused_computation.11.clone.1 | convolution fusion | flops 168689664 | bytes 986112 | tf_op jit(solution)/shard_map/while/body/eval_jaxpr/dot_general | solution.py:9
  92.0 1.6 %multiply_convert_fusion.6 = bf16[256,512]{1,0:T(8,128)(2,1)S(1)} fusion(bf16[1,512,512]{2,1,0:T(8,128)(2,1)} %get-tuple-element.400, f32[512]{0:T(512)S(1)} %bitcast.71, bf16[16,128,512]{2,1,0:T(8,128)(2,1)} %get-tuple-element.399, s32[]{:T(128)S(6)} %select_n.74, bf16[16,256,128]{2,1,0:T(8,128)(2,1)} %get-tuple-element.398), kind=kOutput, calls=%fused_computation.11.clone.1 | convolution fusion | flops 168689664 | bytes 986112 | tf_op jit(solution)/shard_map/while/body/eval_jaxpr/dot_general | solution.py:9
  95.1 1.6 %multiply_convert_fusion.6 = bf16[256,512]{1,0:T(8,128)(2,1)S(1)} fusion(bf16[1,512,512]{2,1,0:T(8,128)(2,1)} %get-tuple-element.400, f32[512]{0:T(512)S(1)} %bitcast.71, bf16[16,128,512]{2,1,0:T(8,128)(2,1)} %get-tuple-element.399, s32[]{:T(128)S(6)} %select_n.74, bf16[16,256,128]{2,1,0:T(8,128)(2,1)} %get-tuple-element.398), kind=kOutput, calls=%fused_computation.11.clone.1 | convolution fusion | flops 168689664 | bytes 986112 | tf_op jit(solution)/shard_map/while/body/eval_jaxpr/dot_general | solution.py:9
  97.4 0.9 fusion.35
  98.3 1.6 %multiply_convert_fusion.6 = bf16[256,512]{1,0:T(8,128)(2,1)S(1)} fusion(bf16[1,512,512]{2,1,0:T(8,128)(2,1)} %get-tuple-element.400, f32[512]{0:T(512)S(1)} %bitcast.71, bf16[16,128,512]{2,1,0:T(8,128)(2,1)} %get-tuple-element.399, s32[]{:T(128)S(6)} %select_n.74, bf16[16,256,128]{2,1,0:T(8,128)(2,1)} %get-tuple-element.398), kind=kOutput, calls=%fused_computation.11.clone.1 | convolution fusion | flops 168689664 | bytes 986112 | tf_op jit(solution)/shard_map/while/body/eval_jaxpr/dot_general | solution.py:9
  101.4 1.6 %multiply_convert_fusion.6 = bf16[256,512]{1,0:T(8,128)(2,1)S(1)} fusion(bf16[1,512,512]{2,1,0:T(8,128)(2,1)} %get-tuple-element.400, f32[512]{0:T(512)S(1)} %bitcast.71, bf16[16,128,512]{2,1,0:T(8,128)(2,1)} %get-tuple-element.399, s32[]{:T(128)S(6)} %select_n.74, bf16[16,256,128]{2,1,0:T(8,128)(2,1)} %get-tuple-element.398), kind=kOutput, calls=%fused_computation.11.clone.1 | convolution fusion | flops 168689664 | bytes 986112 | tf_op jit(solution)/shard_map/while/body/eval_jaxpr/dot_general | solution.py:9
  104.6 1.6 %multiply_convert_fusion.6 = bf16[256,512]{1,0:T(8,128)(2,1)S(1)} fusion(bf16[1,512,512]{2,1,0:T(8,128)(2,1)} %get-tuple-element.400, f32[512]{0:T(512)S(1)} %bitcast.71, bf16[16,128,512]{2,1,0:T(8,128)(2,1)} %get-tuple-element.399, s32[]{:T(128)S(6)} %select_n.74, bf16[16,256,128]{2,1,0:T(8,128)(2,1)} %get-tuple-element.398), kind=kOutput, calls=%fused_computation.11.clone.1 | convolution fusion | flops 168689664 | bytes 986112 | tf_op jit(solution)/shard_map/while/body/eval_jaxpr/dot_general | solution.py:9
  107.7 1.6 %multiply_convert_fusion.6 = bf16[256,512]{1,0:T(8,128)(2,1)S(1)} fusion(bf16[1,512,512]{2,1,0:T(8,128)(2,1)} %get-tuple-element.400, f32[512]{0:T(512)S(1)} %bitcast.71, bf16[16,128,512]{2,1,0:T(8,128)(2,1)} %get-tuple-element.399, s32[]{:T(128)S(6)} %select_n.74, bf16[16,256,128]{2,1,0:T(8,128)(2,1)} %get-tuple-element.398), kind=kOutput, calls=%fused_computation.11.clone.1 | convolution fusion | flops 168689664 | bytes 986112 | tf_op jit(solution)/shard_map/while/body/eval_jaxpr/dot_general | solution.py:9
  110.8 1.6 %multiply_convert_fusion.6 = bf16[256,512]{1,0:T(8,128)(2,1)S(1)} fusion(bf16[1,512,512]{2,1,0:T(8,128)(2,1)} %get-tuple-element.400, f32[512]{0:T(512)S(1)} %bitcast.71, bf16[16,128,512]{2,1,0:T(8,128)(2,1)} %get-tuple-element.399, s32[]{:T(128)S(6)} %select_n.74, bf16[16,256,128]{2,1,0:T(8,128)(2,1)} %get-tuple-element.398), kind=kOutput, calls=%fused_computation.11.clone.1 | convolution fusion | flops 168689664 | bytes 986112 | tf_op jit(solution)/shard_map/while/body/eval_jaxpr/dot_general | solution.py:9
  113.1 0.9 fusion.35
  114.0 1.7 %multiply_convert_fusion.6 = bf16[256,512]{1,0:T(8,128)(2,1)S(1)} fusion(bf16[1,512,512]{2,1,0:T(8,128)(2,1)} %get-tuple-element.400, f32[512]{0:T(512)S(1)} %bitcast.71, bf16[16,128,512]{2,1,0:T(8,128)(2,1)} %get-tuple-element.399, s32[]{:T(128)S(6)} %select_n.74, bf16[16,256,128]{2,1,0:T(8,128)(2,1)} %get-tuple-element.398), kind=kOutput, calls=%fused_computation.11.clone.1 | convolution fusion | flops 168689664 | bytes 986112 | tf_op jit(solution)/shard_map/while/body/eval_jaxpr/dot_general | solution.py:9
  117.1 1.6 %multiply_convert_fusion.6 = bf16[256,512]{1,0:T(8,128)(2,1)S(1)} fusion(bf16[1,512,512]{2,1,0:T(8,128)(2,1)} %get-tuple-element.400, f32[512]{0:T(512)S(1)} %bitcast.71, bf16[16,128,512]{2,1,0:T(8,128)(2,1)} %get-tuple-element.399, s32[]{:T(128)S(6)} %select_n.74, bf16[16,256,128]{2,1,0:T(8,128)(2,1)} %get-tuple-element.398), kind=kOutput, calls=%fused_computation.11.clone.1 | convolution fusion | flops 168689664 | bytes 986112 | tf_op jit(solution)/shard_map/while/body/eval_jaxpr/dot_general | solution.py:9
  120.2 1.6 %multiply_convert_fusion.6 = bf16[256,512]{1,0:T(8,128)(2,1)S(1)} fusion(bf16[1,512,512]{2,1,0:T(8,128)(2,1)} %get-tuple-element.400, f32[512]{0:T(512)S(1)} %bitcast.71, bf16[16,128,512]{2,1,0:T(8,128)(2,1)} %get-tuple-element.399, s32[]{:T(128)S(6)} %select_n.74, bf16[16,256,128]{2,1,0:T(8,128)(2,1)} %get-tuple-element.398), kind=kOutput, calls=%fused_computation.11.clone.1 | convolution fusion | flops 168689664 | bytes 986112 | tf_op jit(solution)/shard_map/while/body/eval_jaxpr/dot_general | solution.py:9
  123.4 1.6 %multiply_convert_fusion.6 = bf16[256,512]{1,0:T(8,128)(2,1)S(1)} fusion(bf16[1,512,512]{2,1,0:T(8,128)(2,1)} %get-tuple-element.400, f32[512]{0:T(512)S(1)} %bitcast.71, bf16[16,128,512]{2,1,0:T(8,128)(2,1)} %get-tuple-element.399, s32[]{:T(128)S(6)} %select_n.74, bf16[16,256,128]{2,1,0:T(8,128)(2,1)} %get-tuple-element.398), kind=kOutput, calls=%fused_computation.11.clone.1 | convolution fusion | flops 168689664 | bytes 986112 | tf_op jit(solution)/shard_map/while/body/eval_jaxpr/dot_general | solution.py:9
  126.5 9.4 %all_to_all.15 = f32[12,16,256]{2,0,1:T(8,128)S(1)} all-to-all(f32[12,16,256]{2,0,1:T(8,128)} %get-tuple-element.270), channel_id=1, replica_groups=mesh['band'=8,'patch'=4] {'patch'}, dimensions={1} | all-to-all | bytes 393216 | tf_op jit(solution)/shard_map/all_to_all | solution.py:67
  136.0 0.9 broadcast_in_dim_reshape.3
  (105 shorter events, 25.0 us)
Async XLA Ops:
  7.4 1.8 %copy-start = (bf16[1,2560,512]{2,1,0:T(8,128)(2,1)S(1)}, bf16[1,2560,512]{2,1,0:T(8,128)(2,1)}, u32[]{:S(2)}) copy-start(bf16[1,2560,512]{2,1,0:T(8,128)(2,1)} %param.13) | copy-start | bytes 7864324
  7.4 68.2 %all-reduce.2.cloned.1.call-start = ((), (), s32[]{:S(2)}) async-start(), calls=%async_computation.2 | async-start | bytes 4194304 | tf_op jit(solution)/shard_map/psum | solution.py:58
  9.1 9.2 %copy-start.7 = (s32[16]{0:T(128)S(1)}, s32[16]{0:T(128)}, u32[]{:S(2)}) copy-start(s32[16]{0:T(128)} %param.14) | copy-start | bytes 196
  21.2 55.1 %copy-start.1 = (bf16[1,512,512]{2,1,0:T(8,128)(2,1)S(1)}, bf16[1,512,512]{2,1,0:T(8,128)(2,1)}, u32[]{:S(2)}) copy-start(bf16[1,512,512]{2,1,0:T(8,128)(2,1)} %param.19) | copy-start | bytes 1572868
  21.2 55.1 %copy-start.2 = (bf16[1,12,512]{2,1,0:T(8,128)(2,1)S(1)}, bf16[1,12,512]{2,1,0:T(8,128)(2,1)}, u32[]{:S(2)}) copy-start(bf16[1,12,512]{2,1,0:T(8,128)(2,1)} %param.22) | copy-start | bytes 36868
  21.2 55.1 %copy-start.3 = (f32[1,512]{1,0:T(1,128)S(1)}, f32[1,512]{1,0:T(1,128)}, u32[]{:S(2)}) copy-start(f32[1,512]{1,0:T(1,128)} %param.20) | copy-start | bytes 6148
  21.2 55.1 %copy-start.4 = (f32[1,512]{1,0:T(1,128)S(1)}, f32[1,512]{1,0:T(1,128)}, u32[]{:S(2)}) copy-start(f32[1,512]{1,0:T(1,128)} %param.21) | copy-start | bytes 6148
  21.2 55.1 %copy-start.5 = (f32[1,12]{1,0:T(1,128)S(1)}, f32[1,12]{1,0:T(1,128)}, u32[]{:S(2)}) copy-start(f32[1,12]{1,0:T(1,128)} %param.23) | copy-start | bytes 148
  21.2 55.1 %copy-start.6 = (f32[1,512]{1,0:T(1,128)S(1)}, f32[1,512]{1,0:T(1,128)}, u32[]{:S(2)}) copy-start(f32[1,512]{1,0:T(1,128)} %param.18) | copy-start | bytes 6148
  21.3 54.3 %all-gather.2.cloned.1.call-start = ((), (), s32[]{:S(2)}) async-start(), calls=%async_computation.1 | async-start | bytes 1179648 | tf_op jit(solution)/shard_map/all_gather | solution.py:40
Sparse Core Ops, SparseCore 0:
  21.4 54.1 all-reduce.1
Sparse Core Ops, SparseCore 1:
  23.9 43.0 all-gather.1
where the time goes:
time: 145 us; the launch traced here: 144 us
  waiting for transfers between devices  54.2 us (37%)
  matrix products  46.4 us (32%)
  between operations  14.9 us (10%)
  local copies, waits for them, and re-layouts  11.2 us (8%)
  blocking collectives  9.38 us (6%)
  other arithmetic  7.95 us (5%)
    psum x1, waiting for transfers between devices, body(): all_blocks = lax.psum(filled.astype(jnp.bfloat16), 'patch')  53.7 us
    dot_general x16, matrix products, decode_rows(): jnp.dot(interp, w_first, preferred_element_type=jnp.float32) + b_first  26.3 us
    dot_general x16, matrix products, decode_rows(): lax.dot_general(w_out, normed, (((1,), (1,)), ((), ())), preferred_elemen...  13.9 us
    all_to_all x1, blocking collectives, body(): lax.all_to_all(decoded, 'patch', split_axis=1, concat_axis=2, tiled=True)  9.38 us
    gather x1, local copies, waits for them, and re-layouts, body(): jnp.take(local_latents, block_rows.reshape(-1), axis=0)  9.18 us
    dot_general x16, matrix products, decode_rows(): jnp.dot(hidden, w_second, preferred_element_type=jnp.float32) + b_second  6.16 us
    reduce_sum x16, other arithmetic, decode_rows(): variance = jnp.mean(centred * centred, axis=-1, keepdims=True)  3.28 us
    convert_element_type x1, other arithmetic, body(): all_blocks = lax.psum(filled.astype(jnp.bfloat16), 'patch')  2.9 us
  transfers between devices with their start and end apart: 2, of which 1 were waited for; matrix products, arithmetic and copies ran while one was open for 0% of the time, Pallas kernels for 0%

commit v1 on v0

--- a/solution.py
+++ b/solution.py
@@ -64,7 +64,12 @@
         return lax.dynamic_update_index_in_dim(buffer, result, tile_index, 1)
 
     decoded = lax.fori_loop(0, tile_count, visit_summed, empty)
-    regrid = lax.all_to_all(decoded, "patch", split_axis=1, concat_axis=2, tiled=True)
+    regrid = jnp.concatenate(
+        lax.all_to_all(
+            jnp.stack(jnp.split(decoded, lax.axis_size("patch"), axis=1)), "patch", 0, 0
+        ),
+        axis=2,
+    )
     return regrid.reshape(channels, -1)[None]
 
 

time: 145 us -> 161 us (1.11)
  local copies, waits for them, and re-layouts: 11.2 us -> 37.9 us
  matrix products: 46.4 us -> 36.7 us
  blocking collectives: 9.38 us -> 7.67 us
    dynamic_update_slice x0 -> x32, local copies, waits for them, and re-layouts: none -> 25.6 us  [visit_summed(): return lax.dynamic_update_index_in_dim(buffer, result, tile_index, 1)]
    dot_general x16, matrix products: 13.9 us -> 4.14 us  [decode_rows(): lax.dot_general(w_out, normed, (((1,), (1,)), ((), ())), preferred_elemen...]
    all_to_all x1, blocking collectives: 9.38 us -> 7.67 us  [body(): lax.all_to_all(jnp.stack(jnp.split(decoded, lax.axis_size('patch'), axis=...]
where the time goes in v1:
time: 161 us; the launch traced here: 160 us
  waiting for transfers between devices  54.2 us (34%)
  local copies, waits for them, and re-layouts  37.9 us (24%)
  matrix products  36.7 us (23%)
  between operations  14.9 us (9%)
  other arithmetic  7.99 us (5%)
  blocking collectives  7.67 us (5%)
    psum x1, waiting for transfers between devices, body(): all_blocks = lax.psum(filled.astype(jnp.bfloat16), 'patch')  53.7 us
    dot_general x16, matrix products, decode_rows(): jnp.dot(interp, w_first, preferred_element_type=jnp.float32) + b_first  26.4 us
    dynamic_update_slice x32, local copies, waits for them, and re-layouts, visit_summed(): return lax.dynamic_update_index_in_dim(buffer, result, tile_index, 1)  25.6 us
    gather x1, local copies, waits for them, and re-layouts, body(): jnp.take(local_latents, block_rows.reshape(-1), axis=0)  9.21 us
    all_to_all x1, blocking collectives, body(): lax.all_to_all(jnp.stack(jnp.split(decoded, lax.axis_size('patch'), axis=...  7.67 us
    dot_general x16, matrix products, decode_rows(): jnp.dot(hidden, w_second, preferred_element_type=jnp.float32) + b_second  6.16 us
    dot_general x16, matrix products, decode_rows(): lax.dot_general(w_out, normed, (((1,), (1,)), ((), ())), preferred_elemen...  4.14 us
    reduce_sum x16, other arithmetic, decode_rows(): variance = jnp.mean(centred * centred, axis=-1, keepdims=True)  3.28 us
  transfers between devices with their start and end apart: 2, of which 1 were waited for; matrix products, arithmetic and copies ran while one was open for 0% of the time, Pallas kernels for 0%

profile of v1, /device:TPU:0, one launch (start us, length us, event | category | flops | bytes accessed | tf_op | source)
XLA Modules:
  0.0 159.9 jit_solution(8485834692615193543)
XLA Ops:
  9.1 9.2 %gather_fusion = bf16[2048,512]{1,0:T(8,128)(2,1)} fusion(bf16[2560,512]{1,0:T(8,128)(2,1)S(1)} %bitcast.65, s32[2048]{0:T(1024)S(1)} %broadcast_clamp_fusion), kind=kCustom, calls=%fused_computation | custom fusion | bytes 4202496 | tf_op jit(solution)/shard_map/jit(_take)/gather | solution.py:53
  18.3 2.9 %select_convert_fusion = bf16[16,128,512]{2,1,0:T(8,128)(2,1)} fusion(bf16[16,128,512]{2,1,0:T(8,128)(2,1)} %bitcast.66, pred[16]{0:T(512)(128)(4,1)S(1)} %broadcast_compare_fusion, pred[16,128]{1,0:T(8,128)(4,1)S(1)} %compare_and_fusion), kind=kLoop, calls=%fused_computation.22 | loop fusion | flops 4194304 | bytes 4196368 | tf_op jit(solution)/shard_map/convert_element_type | solution.py:58
  21.9 53.7 %all-reduce.2.cloned.1.call-done = bf16[16,128,512]{2,1,0:T(8,128)(2,1)} async-done(((bf16[16,128,512]{2,1,0:T(8,128)(2,1)}), bf16[16,128,512]{2,1,0:T(8,128)(2,1)}) %all-reduce.2.cloned.1.call-update) | async-done | bytes 2097168 | tf_op jit(solution)/shard_map/psum | solution.py:58
  76.3 66.3 %while.15 = (s32[]{:T(128)}, f32[12,16,256]{2,1,0:T(8,128)}, bf16[16,256,128]{2,1,0:T(8,128)(2,1)}, bf16[16,128,512]{2,1,0:T(8,128)(2,1)}, bf16[1,512,512]{2,1,0...) while((s32[]{:T(128)}, f32[12,16,256]{2,1,0:T(8,128)}, ...), condition=%wide.region_4.5_spmd, body=%wide.region_1.4_spmd.sunk | while | flops 307236096 | bytes 3432733 | solution.py:66
  76.3 1.7 %multiply_convert_fusion.6 = bf16[256,512]{1,0:T(8,128)(2,1)S(1)} fusion(bf16[1,512,512]{2,1,0:T(8,128)(2,1)} %get-tuple-element.404, f32[512]{0:T(512)S(1)} %bitcast.73, bf16[16,128,512]{2,1,0:T(8,128)(2,1)} %get-tuple-element.403, s32[]{:T(128)S(6)} %select_n.74, bf16[16,256,128]{2,1,0:T(8,128)(2,1)} %get-tuple-element.402), kind=kOutput, calls=%fused_computation.10.clone.1 | convolution fusion | flops 168689664 | bytes 986112 | tf_op jit(solution)/shard_map/while/body/eval_jaxpr/dot_general | solution.py:9
  80.5 1.6 %multiply_convert_fusion.6 = bf16[256,512]{1,0:T(8,128)(2,1)S(1)} fusion(bf16[1,512,512]{2,1,0:T(8,128)(2,1)} %get-tuple-element.404, f32[512]{0:T(512)S(1)} %bitcast.73, bf16[16,128,512]{2,1,0:T(8,128)(2,1)} %get-tuple-element.403, s32[]{:T(128)S(6)} %select_n.74, bf16[16,256,128]{2,1,0:T(8,128)(2,1)} %get-tuple-element.402), kind=kOutput, calls=%fused_computation.10.clone.1 | convolution fusion | flops 168689664 | bytes 986112 | tf_op jit(solution)/shard_map/while/body/eval_jaxpr/dot_general | solution.py:9
  83.0 1.6 dynamic_update_slice.12
  84.6 1.6 %multiply_convert_fusion.6 = bf16[256,512]{1,0:T(8,128)(2,1)S(1)} fusion(bf16[1,512,512]{2,1,0:T(8,128)(2,1)} %get-tuple-element.404, f32[512]{0:T(512)S(1)} %bitcast.73, bf16[16,128,512]{2,1,0:T(8,128)(2,1)} %get-tuple-element.403, s32[]{:T(128)S(6)} %select_n.74, bf16[16,256,128]{2,1,0:T(8,128)(2,1)} %get-tuple-element.402), kind=kOutput, calls=%fused_computation.10.clone.1 | convolution fusion | flops 168689664 | bytes 986112 | tf_op jit(solution)/shard_map/while/body/eval_jaxpr/dot_general | solution.py:9
  87.2 1.6 dynamic_update_slice.12
  88.7 1.7 %multiply_convert_fusion.6 = bf16[256,512]{1,0:T(8,128)(2,1)S(1)} fusion(bf16[1,512,512]{2,1,0:T(8,128)(2,1)} %get-tuple-element.404, f32[512]{0:T(512)S(1)} %bitcast.73, bf16[16,128,512]{2,1,0:T(8,128)(2,1)} %get-tuple-element.403, s32[]{:T(128)S(6)} %select_n.74, bf16[16,256,128]{2,1,0:T(8,128)(2,1)} %get-tuple-element.402), kind=kOutput, calls=%fused_computation.10.clone.1 | convolution fusion | flops 168689664 | bytes 986112 | tf_op jit(solution)/shard_map/while/body/eval_jaxpr/dot_general | solution.py:9
  91.3 1.6 dynamic_update_slice.12
  92.9 1.7 %multiply_convert_fusion.6 = bf16[256,512]{1,0:T(8,128)(2,1)S(1)} fusion(bf16[1,512,512]{2,1,0:T(8,128)(2,1)} %get-tuple-element.404, f32[512]{0:T(512)S(1)} %bitcast.73, bf16[16,128,512]{2,1,0:T(8,128)(2,1)} %get-tuple-element.403, s32[]{:T(128)S(6)} %select_n.74, bf16[16,256,128]{2,1,0:T(8,128)(2,1)} %get-tuple-element.402), kind=kOutput, calls=%fused_computation.10.clone.1 | convolution fusion | flops 168689664 | bytes 986112 | tf_op jit(solution)/shard_map/while/body/eval_jaxpr/dot_general | solution.py:9
  97.0 1.7 %multiply_convert_fusion.6 = bf16[256,512]{1,0:T(8,128)(2,1)S(1)} fusion(bf16[1,512,512]{2,1,0:T(8,128)(2,1)} %get-tuple-element.404, f32[512]{0:T(512)S(1)} %bitcast.73, bf16[16,128,512]{2,1,0:T(8,128)(2,1)} %get-tuple-element.403, s32[]{:T(128)S(6)} %select_n.74, bf16[16,256,128]{2,1,0:T(8,128)(2,1)} %get-tuple-element.402), kind=kOutput, calls=%fused_computation.10.clone.1 | convolution fusion | flops 168689664 | bytes 986112 | tf_op jit(solution)/shard_map/while/body/eval_jaxpr/dot_general | solution.py:9
  101.2 1.7 %multiply_convert_fusion.6 = bf16[256,512]{1,0:T(8,128)(2,1)S(1)} fusion(bf16[1,512,512]{2,1,0:T(8,128)(2,1)} %get-tuple-element.404, f32[512]{0:T(512)S(1)} %bitcast.73, bf16[16,128,512]{2,1,0:T(8,128)(2,1)} %get-tuple-element.403, s32[]{:T(128)S(6)} %select_n.74, bf16[16,256,128]{2,1,0:T(8,128)(2,1)} %get-tuple-element.402), kind=kOutput, calls=%fused_computation.10.clone.1 | convolution fusion | flops 168689664 | bytes 986112 | tf_op jit(solution)/shard_map/while/body/eval_jaxpr/dot_general | solution.py:9
  105.3 1.7 %multiply_convert_fusion.6 = bf16[256,512]{1,0:T(8,128)(2,1)S(1)} fusion(bf16[1,512,512]{2,1,0:T(8,128)(2,1)} %get-tuple-element.404, f32[512]{0:T(512)S(1)} %bitcast.73, bf16[16,128,512]{2,1,0:T(8,128)(2,1)} %get-tuple-element.403, s32[]{:T(128)S(6)} %select_n.74, bf16[16,256,128]{2,1,0:T(8,128)(2,1)} %get-tuple-element.402), kind=kOutput, calls=%fused_computation.10.clone.1 | convolution fusion | flops 168689664 | bytes 986112 | tf_op jit(solution)/shard_map/while/body/eval_jaxpr/dot_general | solution.py:9
  109.5 1.7 %multiply_convert_fusion.6 = bf16[256,512]{1,0:T(8,128)(2,1)S(1)} fusion(bf16[1,512,512]{2,1,0:T(8,128)(2,1)} %get-tuple-element.404, f32[512]{0:T(512)S(1)} %bitcast.73, bf16[16,128,512]{2,1,0:T(8,128)(2,1)} %get-tuple-element.403, s32[]{:T(128)S(6)} %select_n.74, bf16[16,256,128]{2,1,0:T(8,128)(2,1)} %get-tuple-element.402), kind=kOutput, calls=%fused_computation.10.clone.1 | convolution fusion | flops 168689664 | bytes 986112 | tf_op jit(solution)/shard_map/while/body/eval_jaxpr/dot_general | solution.py:9
  113.6 1.6 %multiply_convert_fusion.6 = bf16[256,512]{1,0:T(8,128)(2,1)S(1)} fusion(bf16[1,512,512]{2,1,0:T(8,128)(2,1)} %get-tuple-element.404, f32[512]{0:T(512)S(1)} %bitcast.73, bf16[16,128,512]{2,1,0:T(8,128)(2,1)} %get-tuple-element.403, s32[]{:T(128)S(6)} %select_n.74, bf16[16,256,128]{2,1,0:T(8,128)(2,1)} %get-tuple-element.402), kind=kOutput, calls=%fused_computation.10.clone.1 | convolution fusion | flops 168689664 | bytes 986112 | tf_op jit(solution)/shard_map/while/body/eval_jaxpr/dot_general | solution.py:9
  117.7 1.6 %multiply_convert_fusion.6 = bf16[256,512]{1,0:T(8,128)(2,1)S(1)} fusion(bf16[1,512,512]{2,1,0:T(8,128)(2,1)} %get-tuple-element.404, f32[512]{0:T(512)S(1)} %bitcast.73, bf16[16,128,512]{2,1,0:T(8,128)(2,1)} %get-tuple-element.403, s32[]{:T(128)S(6)} %select_n.74, bf16[16,256,128]{2,1,0:T(8,128)(2,1)} %get-tuple-element.402), kind=kOutput, calls=%fused_computation.10.clone.1 | convolution fusion | flops 168689664 | bytes 986112 | tf_op jit(solution)/shard_map/while/body/eval_jaxpr/dot_general | solution.py:9
  121.9 1.6 %multiply_convert_fusion.6 = bf16[256,512]{1,0:T(8,128)(2,1)S(1)} fusion(bf16[1,512,512]{2,1,0:T(8,128)(2,1)} %get-tuple-element.404, f32[512]{0:T(512)S(1)} %bitcast.73, bf16[16,128,512]{2,1,0:T(8,128)(2,1)} %get-tuple-element.403, s32[]{:T(128)S(6)} %select_n.74, bf16[16,256,128]{2,1,0:T(8,128)(2,1)} %get-tuple-element.402), kind=kOutput, calls=%fused_computation.10.clone.1 | convolution fusion | flops 168689664 | bytes 986112 | tf_op jit(solution)/shard_map/while/body/eval_jaxpr/dot_general | solution.py:9
  126.0 1.6 %multiply_convert_fusion.6 = bf16[256,512]{1,0:T(8,128)(2,1)S(1)} fusion(bf16[1,512,512]{2,1,0:T(8,128)(2,1)} %get-tuple-element.404, f32[512]{0:T(512)S(1)} %bitcast.73, bf16[16,128,512]{2,1,0:T(8,128)(2,1)} %get-tuple-element.403, s32[]{:T(128)S(6)} %select_n.74, bf16[16,256,128]{2,1,0:T(8,128)(2,1)} %get-tuple-element.402), kind=kOutput, calls=%fused_computation.10.clone.1 | convolution fusion | flops 168689664 | bytes 986112 | tf_op jit(solution)/shard_map/while/body/eval_jaxpr/dot_general | solution.py:9
  130.1 1.6 %multiply_convert_fusion.6 = bf16[256,512]{1,0:T(8,128)(2,1)S(1)} fusion(bf16[1,512,512]{2,1,0:T(8,128)(2,1)} %get-tuple-element.404, f32[512]{0:T(512)S(1)} %bitcast.73, bf16[16,128,512]{2,1,0:T(8,128)(2,1)} %get-tuple-element.403, s32[]{:T(128)S(6)} %select_n.74, bf16[16,256,128]{2,1,0:T(8,128)(2,1)} %get-tuple-element.402), kind=kOutput, calls=%fused_computation.10.clone.1 | convolution fusion | flops 168689664 | bytes 986112 | tf_op jit(solution)/shard_map/while/body/eval_jaxpr/dot_general | solution.py:9
  134.3 1.7 %multiply_convert_fusion.6 = bf16[256,512]{1,0:T(8,128)(2,1)S(1)} fusion(bf16[1,512,512]{2,1,0:T(8,128)(2,1)} %get-tuple-element.404, f32[512]{0:T(512)S(1)} %bitcast.73, bf16[16,128,512]{2,1,0:T(8,128)(2,1)} %get-tuple-element.403, s32[]{:T(128)S(6)} %select_n.74, bf16[16,256,128]{2,1,0:T(8,128)(2,1)} %get-tuple-element.402), kind=kOutput, calls=%fused_computation.10.clone.1 | convolution fusion | flops 168689664 | bytes 986112 | tf_op jit(solution)/shard_map/while/body/eval_jaxpr/dot_general | solution.py:9
  138.4 1.7 %multiply_convert_fusion.6 = bf16[256,512]{1,0:T(8,128)(2,1)S(1)} fusion(bf16[1,512,512]{2,1,0:T(8,128)(2,1)} %get-tuple-element.404, f32[512]{0:T(512)S(1)} %bitcast.73, bf16[16,128,512]{2,1,0:T(8,128)(2,1)} %get-tuple-element.403, s32[]{:T(128)S(6)} %select_n.74, bf16[16,256,128]{2,1,0:T(8,128)(2,1)} %get-tuple-element.402), kind=kOutput, calls=%fused_computation.10.clone.1 | convolution fusion | flops 168689664 | bytes 986112 | tf_op jit(solution)/shard_map/while/body/eval_jaxpr/dot_general | solution.py:9
  143.7 7.7 %all_to_all.5 = f32[4,12,4,256]{3,2,1,0:T(4,128)S(1)} all-to-all(f32[4,12,4,256]{3,2,1,0:T(4,128)S(1)} %pad_maximum_fusion), channel_id=1, replica_groups=mesh['band'=8,'patch'=4] {'patch'}, dimensions={0} | all-to-all | bytes 393216 | tf_op jit(solution)/shard_map/all_to_all | solution.py:68
  (139 shorter events, 39.9 us)
Async XLA Ops:
  7.4 1.8 %copy-start = (bf16[1,2560,512]{2,1,0:T(8,128)(2,1)S(1)}, bf16[1,2560,512]{2,1,0:T(8,128)(2,1)}, u32[]{:S(2)}) copy-start(bf16[1,2560,512]{2,1,0:T(8,128)(2,1)} %param.13) | copy-start | bytes 7864324
  7.4 68.2 %all-reduce.2.cloned.1.call-start = ((), (), s32[]{:S(2)}) async-start(), calls=%async_computation.2 | async-start | bytes 4194304 | tf_op jit(solution)/shard_map/psum | solution.py:58
  9.1 9.2 %copy-start.7 = (s32[16]{0:T(128)S(1)}, s32[16]{0:T(128)}, u32[]{:S(2)}) copy-start(s32[16]{0:T(128)} %param.14) | copy-start | bytes 196
  21.2 55.0 %copy-start.1 = (bf16[1,512,512]{2,1,0:T(8,128)(2,1)S(1)}, bf16[1,512,512]{2,1,0:T(8,128)(2,1)}, u32[]{:S(2)}) copy-start(bf16[1,512,512]{2,1,0:T(8,128)(2,1)} %param.19) | copy-start | bytes 1572868
  21.2 55.0 %copy-start.2 = (bf16[1,12,512]{2,1,0:T(8,128)(2,1)S(1)}, bf16[1,12,512]{2,1,0:T(8,128)(2,1)}, u32[]{:S(2)}) copy-start(bf16[1,12,512]{2,1,0:T(8,128)(2,1)} %param.22) | copy-start | bytes 36868
  21.2 55.0 %copy-start.3 = (f32[1,512]{1,0:T(1,128)S(1)}, f32[1,512]{1,0:T(1,128)}, u32[]{:S(2)}) copy-start(f32[1,512]{1,0:T(1,128)} %param.20) | copy-start | bytes 6148
  21.3 55.0 %copy-start.4 = (f32[1,512]{1,0:T(1,128)S(1)}, f32[1,512]{1,0:T(1,128)}, u32[]{:S(2)}) copy-start(f32[1,512]{1,0:T(1,128)} %param.21) | copy-start | bytes 6148
  21.3 55.0 %copy-start.5 = (f32[1,12]{1,0:T(1,128)S(1)}, f32[1,12]{1,0:T(1,128)}, u32[]{:S(2)}) copy-start(f32[1,12]{1,0:T(1,128)} %param.23) | copy-start | bytes 148
  21.3 55.0 %copy-start.6 = (f32[1,512]{1,0:T(1,128)S(1)}, f32[1,512]{1,0:T(1,128)}, u32[]{:S(2)}) copy-start(f32[1,512]{1,0:T(1,128)} %param.18) | copy-start | bytes 6148
  21.3 54.3 %all-gather.2.cloned.1.call-start = ((), (), s32[]{:S(2)}) async-start(), calls=%async_computation.1 | async-start | bytes 1179648 | tf_op jit(solution)/shard_map/all_gather | solution.py:40
Sparse Core Ops, SparseCore 0:
  21.4 54.1 all-reduce.1
Sparse Core Ops, SparseCore 1:
  23.9 43.0 all-gather.1
